TPU v7x, 32 devices: a whole 2x2x4 slice. The times are simulated.
32 devices in a mesh: samp: 4 (over x, core), snp: 8 (over z, y).
Axes of the slice: x: 2, y: 2, z: 4, core: 2. Of those that a mesh axis runs over, the one named last changes fastest.
Arguments:
- genotype: bfloat16 [40960, 40960], P('samp', 'snp'), may hold values from 0 to 2, as said below
- centre: float32 [40960], P('snp'), may hold values from 0.1 to 1
- spread: float32 [40960], P('snp'), may hold values from 0.308 to 0.7072
- pheno_probes: float32 [32, 40960], P(None, ('samp', 'snp')), may hold values from -15.75 to 15.75
Outputs:
- solution: float32 [32, 40960], P(None, ('samp', 'snp'))
- marker_stats: float32 [32, 40960], P(None, 'snp')
Inputs may be any that keep to these rules, and one draw needn't show every extreme that they name: `genotype`: whole numbers.
All inputs are finite; a program needn't handle non-finite values.
Results may differ from a plain program's by a relative error of at most 0.0003.
Values sent between devices are 32-bit elements; how exact they have to be, the bound alone decides.
A program may use at most 448 MiB of HBM per device.

v0:
```python
import math

import jax
import jax.numpy as jnp
from jax import lax
from jax.sharding import PartitionSpec as P

ROUNDS = 3
RIDGE = 0.1
LANES = 128


def split(values):
    high = lax.reduce_precision(values, 8, 7)
    low = lax.reduce_precision(values - high, 8, 7)
    return jnp.concatenate([high, low], axis=0).astype(jnp.bfloat16), high + low


def product(pieces, genotype, dimension):
    rows = pieces.shape[0] // 2
    pieces = lax.dot_general(
        pieces,
        genotype,
        (((1,), (dimension,)), ((), ())),
        preferred_element_type=jnp.float32,
    )
    return pieces[:rows] + pieces[rows:]


def row_sum(values):
    return jnp.sum(values, axis=1, keepdims=True)


def with_scalars(values, scalars):
    rows = values.shape[0]
    filler = jnp.zeros((rows, LANES - len(scalars)), jnp.float32)
    return jnp.concatenate([values, *scalars, filler], axis=1)


def local(samples, markers, genotype, centre, spread, pheno_probes):
    shard = pheno_probes.shape[1]
    columns = genotype.shape[1]
    block = genotype.shape[0]
    first = lax.axis_index("snp") * shard
    inverse = 1.0 / spread[None, :]
    middle = centre[None, :]

    residual = lax.all_gather(pheno_probes, "snp", axis=1, tiled=True)
    direction = load = norm = square = None
    solution = stats = None
    for counter in range(ROUNDS):
        pieces, rounded = split(residual)
        scalars = [row_sum(rounded), row_sum(residual * residual)]
        if counter:
            scalars.append(row_sum(residual * direction))
        raw = product(pieces, genotype, 0)
        total = lax.psum(with_scalars(raw, scalars), "samp")
        residual_load = (total[:, :columns] - total[:, columns : columns + 1] * middle) * inverse
        norm_next = total[:, columns + 1 : columns + 2]
        if counter:
            ratio = norm_next / norm
            cross = total[:, columns + 2 : columns + 3]
            load = residual_load + ratio * load
            direction = residual + ratio * direction
            square = norm_next + 2.0 * ratio * cross + ratio * ratio * square
        else:
            load, direction, square = residual_load, residual, norm_next
        norm = norm_next

        power = row_sum(load * load)
        if counter < ROUNDS - 1:
            pieces, rounded = split(load * inverse)
            image = product(pieces, genotype, 1) - row_sum(rounded * middle)
            summed = lax.psum(with_scalars(image, [power]), "snp")
            power = summed[:, block : block + 1]
        else:
            power = lax.psum(power, "snp")
        step = norm / (power / markers + RIDGE * square)
        own = lax.dynamic_slice_in_dim(direction, first, shard, 1)
        solution = step * own if solution is None else solution + step * own
        stats = step * load if stats is None else stats + step * load
        if counter < ROUNDS - 1:
            applied = summed[:, :block] / markers + RIDGE * direction
            residual = residual - step * applied
    return (solution, stats / math.sqrt(samples))


def solution(mesh):
    in_specs = (P("samp", "snp"), P("snp"), P("snp"), P(None, ("samp", "snp")))
    out_specs = (P(None, ("samp", "snp")), P(None, "snp"))

    def whole(genotype, centre, spread, pheno_probes):
        samples, markers = genotype.shape

        def body(*blocks):
            return local(samples, markers, *blocks)

        return jax.shard_map(
            body, mesh=mesh, in_specs=in_specs, out_specs=out_specs, check_vma=False
        )(genotype, centre, spread, pheno_probes)

    return whole
```

profile of v0, /device:TPU:0, one launch (start us, length us, event | category | flops | bytes accessed | tf_op | source)
XLA Modules:
  0.0 597.3 jit_solution(6193682254995479344)
XLA Ops:
  7.2 0.0 all-gather.2.cloned.1.call-start
  7.2 0.7 all-gather.2.cloned.1.call-update
  7.9 0.0 all-reduce.6.cloned.1.call-start
  7.9 46.8 %all-gather.2.cloned.1.call-done = f32[32,10240]{1,0:T(8,128)} async-done(((f32[32,1280]{1,0:T(8,128)}), f32[32,10240]{1,0:T(8,128)}) %all-gather.2.cloned.1.call-update) | async-done | bytes 1310736 | tf_op jit(solution)/shard_map/all_gather | solution.py:48
  54.7 1.8 multiply_reduce_fusion.4
  56.5 35.8 %fusion.17 = f32[64,5120]{1,0:T(8,128)S(1)} fusion(bf16[10240,5120]{1,0:T(8,128)(2,1)} %param.4, bf16[32,10240]{1,0:T(8,128)(2,1)S(1)} %get-tuple-element.26, bf16[32,10240]{1,0:T(8,128)(2,1)S(1)} %get-tuple-element.27), kind=kOutput, calls=%fused_computation.30 | convolution fusion | flops 6713507840 | bytes 107479040 | tf_op jit(solution)/shard_map/dot_general | solution.py:21
  92.3 0.1 slice_add_fusion.4
  92.4 0.0 copy-start.4
  92.4 0.1 copy.17
  92.5 0.1 copy.18
  92.6 0.9 concatenate.36
  93.5 0.0 all-reduce.6.cloned.1.call-update
  93.5 0.0 all-reduce.8.cloned.1.call-start
  93.6 32.9 %all-reduce.6.cloned.1.call-done = f32[32,5248]{1,0:T(8,128)} async-done(((f32[32,5248]{1,0:T(8,128)}), f32[32,5248]{1,0:T(8,128)}) %all-reduce.6.cloned.1.call-update) | async-done | bytes 671760 | tf_op jit(solution)/shard_map/psum | solution.py:57
  126.4 0.8 slice_reduce_fusion.2
  127.3 1.5 multiply_reduce_fusion.7
  128.8 0.1 copy.19
  128.9 39.7 %fusion.42 = f32[64,10240]{1,0:T(8,128)S(1)} fusion(bf16[10240,5120]{1,0:T(8,128)(2,1)} %param.4, bf16[32,5120]{1,0:T(8,128)(2,1)S(1)} %get-tuple-element.29, bf16[32,5120]{1,0:T(8,128)(2,1)S(1)} %get-tuple-element.28), kind=kOutput, calls=%fused_computation.73 | convolution fusion | flops 6712197120 | bytes 108134400 | tf_op jit(solution)/shard_map/dot_general | solution.py:21
  168.6 1.2 fusion.16
  169.8 2.3 concatenate.38
  172.1 0.0 all-reduce.8.cloned.1.call-update
  172.1 0.0 all-reduce.10.cloned.1.call-start
  172.2 84.1 %all-reduce.8.cloned.1.call-done = f32[32,10368]{1,0:T(8,128)} async-done(((f32[32,10368]{1,0:T(8,128)}), f32[32,10368]{1,0:T(8,128)}) %all-reduce.8.cloned.1.call-update) | async-done | bytes 1327120 | tf_op jit(solution)/shard_map/psum | solution.py:74
  256.3 0.9 fusion.63
  257.2 2.1 multiply_reduce_fusion.2
  259.3 1.0 reduce-precision_convert_fusion.1
  260.3 37.0 %fusion.21 = f32[64,5120]{1,0:T(8,128)} fusion(bf16[10240,5120]{1,0:T(8,128)(2,1)} %param.4, bf16[32,10240]{1,0:T(8,128)(2,1)} %get-tuple-element.25, bf16[32,10240]{1,0:T(8,128)(2,1)S(1)} %get-tuple-element.24), kind=kOutput, calls=%fused_computation.34 | convolution fusion | flops 6713507840 | bytes 107479040 | tf_op jit(solution)/shard_map/dot_general | solution.py:21
  297.3 1.4 slice_add_fusion.3
  298.7 0.1 copy.20
  298.8 0.1 copy.21
  298.9 0.1 copy.22
  299.0 0.9 concatenate.40
  299.9 0.0 all-reduce.10.cloned.1.call-update
  299.9 0.2 all-reduce.12.cloned.1.call-start
  300.1 33.0 %all-reduce.10.cloned.1.call-done = f32[32,5248]{1,0:T(8,128)} async-done(((f32[32,5248]{1,0:T(8,128)}), f32[32,5248]{1,0:T(8,128)}) %all-reduce.10.cloned.1.call-update) | async-done | bytes 671760 | tf_op jit(solution)/shard_map/psum | solution.py:57
  333.1 1.0 slice_reduce_fusion.1
  334.1 1.8 multiply_reduce_fusion.6
  336.0 0.9 reduce-precision_convert_fusion.3
  336.9 0.1 copy.23
  337.0 40.9 %fusion.46 = f32[64,10240]{1,0:T(8,128)} fusion(bf16[10240,5120]{1,0:T(8,128)(2,1)} %param.4, bf16[32,5120]{1,0:T(8,128)(2,1)} %get-tuple-element.31, bf16[32,5120]{1,0:T(8,128)(2,1)} %get-tuple-element.30), kind=kOutput, calls=%fused_computation.77 | convolution fusion | flops 6712197120 | bytes 108134400 | tf_op jit(solution)/shard_map/dot_general | solution.py:21
  377.9 3.0 fusion.12
  380.9 2.3 concatenate.42
  383.1 0.0 all-reduce.12.cloned.1.call-update
  383.2 0.0 all-reduce.14.cloned.1.call-start
  383.2 84.1 %all-reduce.12.cloned.1.call-done = f32[32,10368]{1,0:T(8,128)} async-done(((f32[32,10368]{1,0:T(8,128)}), f32[32,10368]{1,0:T(8,128)}) %all-reduce.12.cloned.1.call-update) | async-done | bytes 1327120 | tf_op jit(solution)/shard_map/psum | solution.py:74
  467.3 1.0 fusion.64
  468.3 3.3 multiply_reduce_fusion
  471.6 1.4 reduce-precision_convert_fusion
  473.0 0.1 copy-done.2
  473.1 36.2 %fusion.25 = f32[64,5120]{1,0:T(8,128)S(1)} fusion(bf16[10240,5120]{1,0:T(8,128)(2,1)} %param.4, bf16[32,10240]{1,0:T(8,128)(2,1)} %get-tuple-element.23, bf16[32,10240]{1,0:T(8,128)(2,1)} %get-tuple-element.22), kind=kOutput, calls=%fused_computation.38 | convolution fusion | flops 6713507840 | bytes 107479040 | tf_op jit(solution)/shard_map/dot_general | solution.py:21
  509.3 0.9 slice_add_fusion.2
  510.2 0.1 copy.24
  510.3 0.1 copy.25
  510.4 0.1 copy.26
  510.5 2.1 concatenate.44
  512.5 0.0 all-reduce.14.cloned.1.call-update
  512.5 33.2 %all-reduce.14.cloned.1.call-done = f32[32,5248]{1,0:T(8,128)} async-done(((f32[32,5248]{1,0:T(8,128)}), f32[32,5248]{1,0:T(8,128)}) %all-reduce.14.cloned.1.call-update) | async-done | bytes 671760 | tf_op jit(solution)/shard_map/psum | solution.py:57
  545.8 1.0 slice_reduce_fusion
  546.7 1.4 multiply_reduce_fusion.5
  548.2 0.1 copy.27
  548.3 37.1 %psum.47 = f32[32,1]{1,0:T(8,128)S(1)} all-reduce(f32[32,1]{1,0:T(8,128)S(1)} %copy.27), channel_id=1, replica_groups=mesh['samp'=4,'snp'=8] {'snp'}, use_global_device_ids=true, to_apply=%region_18.0 | all-reduce | flops 32 | bytes 256 | tf_op jit(solution)/shard_map/psum | solution.py:77
  585.3 1.0 fusion.65
  586.3 2.3 add_multiply_fusion
  588.6 1.8 fusion.51
  (12 shorter events, 0.0 us)
Async XLA Ops:
  7.2 47.5 %all-gather.2.cloned.1.call-start = ((), (), s32[]{:S(2)}) async-start(), calls=%async_computation | async-start | bytes 1474560 | tf_op jit(solution)/shard_map/all_gather | solution.py:48
  7.9 118.5 %all-reduce.6.cloned.1.call-start = ((), (), s32[]{:S(2)}) async-start(), calls=%async_computation.1 | async-start | bytes 1343488 | tf_op jit(solution)/shard_map/psum | solution.py:57
  92.4 1.2 copy-start.4
  92.4 34.9 %copy-start.3 = (f32[5120]{0:T(1024)S(1)}, f32[5120]{0:T(1024)}, u32[]{:S(2)}) copy-start(f32[5120]{0:T(1024)} %param.5) | copy-start | bytes 61444
  93.5 162.8 %all-reduce.8.cloned.1.call-start = ((), (), s32[]{:S(2)}) async-start(), calls=%async_computation.2 | async-start | bytes 2654208 | tf_op jit(solution)/shard_map/psum | solution.py:74
  172.1 85.1 %copy-start = (f32[32,10240]{1,0:T(8,128)S(1)}, f32[32,10240]{1,0:T(8,128)}, u32[]{:S(2)}) copy-start(f32[32,10240]{1,0:T(8,128)} %all-gather.2.cloned.1.call-done) | copy-start | bytes 3932164
  172.1 161.0 %all-reduce.10.cloned.1.call-start = ((), (), s32[]{:S(2)}) async-start(), calls=%async_computation.3 | async-start | bytes 1343488 | tf_op jit(solution)/shard_map/psum | solution.py:57
  299.9 167.4 %all-reduce.12.cloned.1.call-start = ((), (), s32[]{:S(2)}) async-start(), calls=%async_computation.4 | async-start | bytes 2654208 | tf_op jit(solution)/shard_map/psum | solution.py:74
  383.2 162.6 %all-reduce.14.cloned.1.call-start = ((), (), s32[]{:S(2)}) async-start(), calls=%async_computation.5 | async-start | bytes 1343488 | tf_op jit(solution)/shard_map/psum | solution.py:57
  471.6 1.5 copy-start.2
  512.5 72.8 %copy-start.1 = (f32[32,5248]{1,0:T(8,128)S(1)}, f32[32,5248]{1,0:T(8,128)}, u32[]{:S(2)}) copy-start(f32[32,5248]{1,0:T(8,128)} %all-reduce.6.cloned.1.call-done) | copy-start | bytes 2015236
Sparse Core Ops, SparseCore 0:
  10.2 44.5 all-gather.1
  93.6 32.7 all-reduce.5
  172.2 84.0 all-reduce.7
  300.0 33.0 all-reduce.9
  383.3 83.9 all-reduce.11
  512.7 33.0 all-reduce.13
where the time goes:
time: 599 us; the launch traced here: 597 us
  waiting for transfers between devices  315 us (53%)
  matrix products  190 us (32%)
  blocking collectives  37.1 us (6%)
  other arithmetic  30.7 us (5%)
  between operations  14.2 us (2%)
  local copies, waits for them, and re-layouts  10.3 us (2%)
    dot_general x5, matrix products, product(): lax.dot_general(pieces, genotype, (((1,), (dimension,)), ((), ())), prefe...  190 us
    psum x2, waiting for transfers between devices, local(): summed = lax.psum(with_scalars(image, [power]), 'snp')  168 us
    psum x3, waiting for transfers between devices, local(): total = lax.psum(with_scalars(raw, scalars), 'samp')  99.1 us
    all_gather x1, waiting for transfers between devices, local(): residual = lax.all_gather(pheno_probes, 'snp', axis=1, tiled=True)  46.8 us
    psum x1, blocking collectives, local(): power = lax.psum(power, 'snp')  37.1 us
  transfers between devices with their start and end apart: 6, of which 6 were waited for; matrix products, arithmetic and copies ran while one was open for 0% of the time, Pallas kernels for 0%

commit v1 on v0

--- a/solution.py
+++ b/solution.py
@@ -1,8 +1,11 @@
+import functools
 import math
 
 import jax
 import jax.numpy as jnp
 from jax import lax
+from jax.experimental import pallas as pl
+from jax.experimental.pallas import tpu as pltpu
 from jax.sharding import PartitionSpec as P
 
 ROUNDS = 3
@@ -85,6 +88,522 @@
     return (solution, stats / math.sqrt(samples))
 
 
+MESH = pl.DeviceIdType.MESH
+STORED = jnp.float8_e4m3fn
+SLOTS = 7
+FETCHED = 64
+VMEM_LIMIT = 67043328
+
+
+def swap(index, distance, count):
+    result, bit = 0, 1
+    while bit < count:
+        result = result + bit * lax.rem(index // bit + distance // bit, 2)
+        bit *= 2
+    return result
+
+
+def pieces_of(values):
+    high = values.astype(jnp.bfloat16)
+    wide = high.astype(jnp.float32)
+    low = (values - wide).astype(jnp.bfloat16)
+    return high, low, wide + low.astype(jnp.float32)
+
+
+def lanes_sum(values):
+    total = values[:, :LANES]
+    for start in range(LANES, values.shape[1], LANES):
+        total = total + values[:, start : start + LANES]
+    return total
+
+
+def solve(
+    plan,
+    genotype,
+    centre,
+    spread,
+    pheno,
+    solution,
+    stats,
+    stored,
+    stage,
+    pieces,
+    shards,
+    sent,
+    paired,
+    gathered,
+    own_image,
+    loads,
+    crossed,
+    faced,
+    direction,
+    power_sent,
+    power_got,
+    stage_sem,
+    ag_send,
+    ag_recv,
+    y_send,
+    y_recv,
+    z_send,
+    z_recv,
+    c_send,
+    c_recv,
+    x_send,
+    x_recv,
+    lg_send,
+    lg_recv,
+    p_send,
+    p_recv,
+):
+    samples, markers, faces, columns = plan
+    root = math.sqrt(samples)
+    rows = pheno.shape[0]
+    width = pheno.shape[1]
+    part = columns // (2 * faces)
+    depth = shards.shape[0] // 2
+    block_rows = stage.shape[1]
+    samp, snp = lax.axis_index("samp"), lax.axis_index("snp")
+    x, core = samp // 2, lax.rem(samp, 2)
+    z, y = snp // 2, lax.rem(snp, 2)
+
+    def to_snp(zz, yy):
+        return (samp, zz * 2 + yy)
+
+    def to_samp(xx, cc):
+        return (xx * 2 + cc, snp)
+
+    def remote(source, target, send, recv, device):
+        return pltpu.make_async_remote_copy(
+            src_ref=source,
+            dst_ref=target,
+            send_sem=send,
+            recv_sem=recv,
+            device_id=device,
+            device_id_type=MESH,
+        )
+
+    def at(slot):
+        return pl.multiple_of(slot * width, LANES)
+
+    def column(slot):
+        return pl.ds(pl.multiple_of(slot * part, LANES), part)
+
+    def row_range(slot):
+        return pl.ds(at(slot), width)
+
+    lane = lax.broadcasted_iota(jnp.int32, (rows, LANES), 1)
+
+    def packed(*scalars):
+        block = jnp.zeros((rows, LANES), jnp.float32)
+        for position, scalar in enumerate(scalars):
+            block = jnp.where(lane == position, scalar, block)
+        return block
+
+    shards[snp, :, :width] = pheno[...]
+    shards[snp, :, width:] = jnp.zeros((rows, LANES), jnp.float32)
+
+    barrier = pltpu.get_barrier_semaphore()
+    partners = [to_snp(z, 1 - y), to_samp(x, 1 - core)]
+    partners += [to_snp(swap(z, d, depth), y) for d in range(1, depth)]
+    partners += [to_samp(swap(x, d, faces), core) for d in range(1, faces)]
+    for partner in partners:
+        pl.semaphore_signal(barrier, inc=1, device_id=partner, device_id_type=MESH)
+
+    per = width // block_rows
+    blocks = 2 * depth * per
+
+    def shard_at(step):
+        return swap(z, lax.rem(step, depth), depth) * 2 + lax.rem(y + step // depth, 2)
+
+    def fetch(index):
+        slot = lax.rem(index, SLOTS)
+        first = shard_at(index // per) * width + lax.rem(index, per) * block_rows
+        return pltpu.make_async_copy(
+            genotype.at[pl.ds(pl.multiple_of(first, block_rows), block_rows)],
+            stage.at[slot],
+            stage_sem.at[slot],
+        )
+
+    for index in range(SLOTS - 1):
+        fetch(jnp.int32(index)).start()
+    pl.semaphore_wait(barrier, len(partners))
+
+    def own_shard_to(d):
+        device = to_snp(swap(z, d, depth), y) if d else to_snp(z, 1 - y)
+        return remote(shards.at[snp], shards.at[snp], ag_send.at[d], ag_recv.at[snp], device)
+
+    def forward(d):
+        slot = swap(z, d, depth) * 2 + y
+        return remote(
+            shards.at[slot], shards.at[slot], ag_send.at[depth + d], ag_recv.at[slot], to_snp(z, 1 - y)
+        )
+
+    def shard_arrival(slot):
+        return remote(shards.at[slot], shards.at[slot], ag_send.at[0], ag_recv.at[slot], to_snp(z, 1 - y))
+
+    def load_stored(step):
+        def one(q, carry):
+            index = step * per + q
+
+            @pl.when(index + SLOTS - 1 < blocks)
+            def _():
+                fetch(index + SLOTS - 1).start()
+
+            fetch(index).wait()
+            first = shard_at(step) * width + q * block_rows
+            where = pl.ds(pl.multiple_of(first, block_rows), block_rows)
+            stored[where, :] = stage[lax.rem(index, SLOTS)].astype(STORED)
+            return carry
+
+        lax.fori_loop(0, per, one, 0)
+
+    def receive_shard(step):
+        @pl.when(step > 0)
+        def _():
+            shard_arrival(shard_at(step)).wait_recv()
+
+        @pl.when(jnp.logical_and(step > 0, step < depth))
+        def _():
+            forward(step).start()
+
+    def take_shard(slot, sums):
+        values = shards[slot, :, :width]
+        high, low, rounded = pieces_of(values)
+        pieces[slot, :rows, :width] = high
+        pieces[slot, rows:, :width] = low
+        return (
+            sums[0] + lanes_sum(rounded),
+            sums[1] + lanes_sum(values * values),
+            sums[2] + shards[slot, :, width:],
+        )
+
+    def raw_part(slot, target):
+        result = jnp.dot(
+            pieces[slot, :, :width],
+            stored[row_range(slot), column(target)],
+            preferred_element_type=jnp.float32,
+        )
+        sent[target, :, :part] += result[:rows] + result[rows:]
+
+    def core_send(xx):
+        return remote(
+            sent.at[xx * 2 + 1 - core], crossed.at[xx], c_send.at[xx], c_recv.at[xx], to_samp(x, 1 - core)
+        )
+
+    def face_send(xx):
+        return remote(crossed.at[xx], faced.at[x], x_send.at[xx], x_recv.at[x], to_samp(xx, core))
+
+    def face_arrival(xx):
+        return remote(crossed.at[xx], faced.at[xx], x_send.at[xx], x_recv.at[xx], to_samp(xx, core))
+
+    def own_load_to(d):
+        device = to_samp(swap(x, d, faces), core) if d else to_samp(x, 1 - core)
+        return remote(loads.at[samp], loads.at[samp], lg_send.at[d], lg_recv.at[samp], device)
+
+    def load_forward(d):
+        slot = swap(x, d, faces) * 2 + core
+        return remote(
+            loads.at[slot], loads.at[slot], lg_send.at[faces + d], lg_recv.at[slot], to_samp(x, 1 - core)
+        )
+
+    def load_arrival(slot):
+        return remote(loads.at[slot], loads.at[slot], lg_send.at[0], lg_recv.at[slot], to_samp(x, 1 - core))
+
+    def take_load(slot, sums):
+        values = loads[slot]
+        high, low, rounded = pieces_of(values * (1.0 / spread[:, column(slot)]))
+        pieces[slot, :rows, :part] = high
+        pieces[slot, rows:, :part] = low
+        return (
+            sums[0] + lanes_sum(rounded * centre[:, column(slot)]),
+            sums[1] + lanes_sum(values * values),
+        )
+
+    def image_part(slot):
+        result = None
+        for source in range(2 * faces):
+            term = lax.dot_general(
+                pieces[source, :, :part],
+                stored[row_range(slot), source * part : (source + 1) * part],
+                (((1,), (1,)), ((), ())),
+                preferred_element_type=jnp.float32,
+            )
+            result = term if result is None else result + term
+        return result[:rows] + result[rows:]
+
+    def pair_send(zz):
+        return remote(sent.at[zz], paired.at[zz], y_send.at[zz], y_recv.at[zz], to_snp(z, 1 - y))
+
+    def far_send(zz):
+        return remote(paired.at[zz], gathered.at[z], z_send.at[zz], z_recv.at[z], to_snp(zz, y))
+
+    def far_arrival(zz):
+        return remote(paired.at[zz], gathered.at[zz], z_send.at[zz], z_recv.at[zz], to_snp(zz, y))
+
+    norm = square = None
+    for counter in range(ROUNDS):
+        for d in range(depth):
+            own_shard_to(d).start()
+        if counter:
+            for slot in range(2 * faces):
+                where = slice(slot * part, (slot + 1) * part)
+                update = step * loads[slot]
+                stats[:, where] = update if counter == 1 else stats[:, where] + update
+        sent[...] = jnp.zeros(sent.shape, jnp.float32)
+
+        def one_shard(index, sums, counter=counter):
+            if not counter:
+                load_stored(index)
+            receive_shard(index)
+            slot = shard_at(index)
+            sums = take_shard(slot, sums)
+
+            def one_part(target, carry):
+                raw_part(slot, target)
+                return carry
+
+            lax.fori_loop(0, 2 * faces, one_part, 0)
+            return sums
+
+        empty = jnp.zeros((rows, LANES), jnp.float32)
+        last = 2 * depth - 1
+        sums = lax.fori_loop(0, last, one_shard, (empty, empty, empty))
+        if not counter:
+            load_stored(last)
+        slot = shard_at(last)
+        shard_arrival(slot).wait_recv()
+        sums = take_shard(slot, sums)
+        scalars = packed(row_sum(sums[0]), row_sum(sums[1]), sums[2][:, :1])
+        for target in range(2 * faces):
+            sent[target, :, part:] = scalars
+        order = [swap(x, d, faces) for d in range(faces - 1, -1, -1)]
+        for xx in order:
+            raw_part(slot, xx * 2 + 1 - core)
+            core_send(xx).start()
+        for xx in order:
+            raw_part(slot, xx * 2 + core)
+        for xx in order[:-1]:
+            core_send(xx).wait_recv()
+            crossed[xx] += sent[xx * 2 + core]
+            face_send(xx).start()
+        core_send(x).wait_recv()
+        total = crossed[x] + sent[samp]
+        for xx in order[:-1]:
+            face_arrival(xx).wait_recv()
+            total = total + faced[xx]
+
+        norm_next = total[:, part + 1 : part + 2]
+        load = (total[:, :part] - total[:, part : part + 1] * centre[:, column(samp)]) * (
+            1.0 / spread[:, column(samp)]
+        )
+        if counter:
+            ratio = norm_next / norm
+            cross = total[:, part + 2 : part + 3]
+            load = load + ratio * loads[samp]
+            square = norm_next + 2.0 * ratio * cross + ratio * ratio * square
+            loads[samp] = load
+        else:
+            square = norm_next
+            loads[samp] = load
+        for xx in order[:-1]:
+            face_send(xx).wait_send()
+        for d in range(depth):
+            own_shard_to(d).wait_send()
+        for d in range(1, depth):
+            forward(d).wait_send()
+        for d in range(faces - 1, -1, -1):
+            own_load_to(d).start()
+        if counter:
+            direction[...] = shards[snp, :, :width] + ratio * direction[...]
+        else:
+            direction[...] = shards[snp, :, :width]
+        norm = norm_next
+
+        sums = take_load(samp, (empty, empty))
+        for d in range(1, faces):
+            other = swap(x, d, faces) * 2 + core
+            load_arrival(other).wait_recv()
+            load_forward(d).start()
+            sums = take_load(other, sums)
+        for d in range(faces):
+            other = swap(x, d, faces) * 2 + 1 - core
+            load_arrival(other).wait_recv()
+            sums = take_load(other, sums)
+        power = row_sum(sums[1])
+
+        if counter < ROUNDS - 1:
+            offset = row_sum(sums[0])
+            scalars = packed(power)
+            for xx in order:
+                core_send(xx).wait_send()
+
+            def one_image(index, carry, offset=offset, scalars=scalars):
+                own = jnp.logical_or(
+                    index == 2 * depth - 1, jnp.logical_and(index > 0, lax.rem(index, 2) == 0)
+                )
+                ahead = jnp.where(index == 2 * depth - 1, depth - 1, (index + 1) // 2)
+                rank = jnp.where(
+                    jnp.logical_and(index < 2 * depth - 1, own), index // 2 - 1, ahead
+                )
+                zz = swap(z, depth - 1 - rank, depth)
+                slot = zz * 2 + jnp.where(own, y, 1 - y)
+                own_image[...] = image_part(slot) - offset
+
+                @pl.when(jnp.logical_not(own))
+                def _():
+                    sent[zz, :, :width] = own_image[...]
+                    sent[zz, :, width:] = scalars
+                    pair_send(zz).start()
+
+                @pl.when(own)
+                def _():
+                    pair_send(zz).wait_recv()
+                    paired[zz, :, :width] += own_image[...]
+                    paired[zz, :, width:] += scalars
+
+                @pl.when(jnp.logical_and(own, index < 2 * depth - 1))
+                def _():
+                    far_send(zz).start()
+
+                return carry
+
+            lax.fori_loop(0, 2 * depth, one_image, 0)
+            total = paired[z]
+            for d in range(depth - 1, 0, -1):
+                zz = swap(z, d, depth)
+                far_arrival(zz).wait_recv()
+                total = total + gathered[zz]
+            power = total[:, width : width + 1]
+            step = norm / (power / markers + RIDGE * square)
+            own_direction = direction[...]
+            update = step * own_direction
+            applied = total[:, :width] / markers + RIDGE * own_direction
+            residual = shards[snp, :, :width] - step * applied
+            shards[snp, :, :width] = residual
+            shards[snp, :, width:] = packed(row_sum(residual * own_direction))
+            solution[...] = update if not counter else solution[...] + update
+            for d in range(depth):
+                pair_send(swap(z, d, depth)).wait_send()
+            for d in range(1, depth):
+                far_send(swap(z, d, depth)).wait_send()
+        else:
+            power_sent[0] = jnp.broadcast_to(power, (rows, LANES))
+            swap_power = remote(
+                power_sent.at[0], power_got.at[z], p_send.at[0], p_recv.at[z], to_snp(z, 1 - y)
+            )
+            swap_power.start()
+            swap_power.wait_recv()
+            power_sent[1] = power_sent[0] + power_got[z]
+            total = power_sent[1]
+
+            def spread_power(d, source):
+                return remote(
+                    power_sent.at[1],
+                    power_got.at[source],
+                    p_send.at[d],
+                    p_recv.at[source],
+                    to_snp(swap(z, d, depth), y),
+                )
+
+            for d in range(1, depth):
+                spread_power(d, z).start()
+            for d in range(1, depth):
+                source = swap(z, d, depth)
+                spread_power(d, source).wait_recv()
+                total = total + power_got[source]
+            step = norm / (total[:, :1] / markers + RIDGE * square)
+            solution[...] += step * direction[...]
+            for slot in range(2 * faces):
+                where = slice(slot * part, (slot + 1) * part)
+                stats[:, where] = (stats[:, where] + step * loads[slot]) / root
+            swap_power.wait_send()
+            for d in range(1, depth):
+                spread_power(d, z).wait_send()
+            for xx in order:
+                core_send(xx).wait_send()
+        for d in range(faces):
+            own_load_to(d).wait_send()
+        for d in range(1, faces):
+            load_forward(d).wait_send()
+
+
+def power_of_two(count):
+    return count > 0 and count & (count - 1) == 0
+
+
+def fits(mesh, genotype, pheno_probes):
+    groups, sections = mesh.shape["samp"], mesh.shape["snp"]
+    if groups % 2 or sections % 2 or not power_of_two(groups) or not power_of_two(sections):
+        return False
+    samples, markers = genotype.shape
+    rows = pheno_probes.shape[0]
+    block, columns = samples // groups, markers // sections
+    width, part = block // sections, columns // groups
+    if rows % 16 or width % LANES or width != part or sections // 2 < groups or groups < 4:
+        return False
+    shard = rows * (width + LANES) * 4
+    used = block * columns + SLOTS * FETCHED * columns * 2 + sections * rows * width * 4
+    used += (sections + 3 * sections // 2 + 2 * groups + 6) * shard
+    return used < VMEM_LIMIT
+
+
+def resident(samples, markers, groups, sections, genotype, centre, spread, pheno_probes):
+    rows, width = pheno_probes.shape
+    block, columns = genotype.shape
+    faces, depth = groups // 2, sections // 2
+    part = columns // groups
+    message = (rows, width + LANES)
+    f32 = jnp.float32
+    dma = pltpu.SemaphoreType.DMA
+    flops = 2 * (2 * ROUNDS - 1) * 2 * rows * block * columns
+    return pl.pallas_call(
+        functools.partial(solve, (samples, markers, faces, columns)),
+        out_shape=(
+            jax.ShapeDtypeStruct((rows, width), f32),
+            jax.ShapeDtypeStruct((rows, columns), f32),
+        ),
+        in_specs=[pl.BlockSpec(memory_space=pl.ANY)] + [pl.BlockSpec(memory_space=pltpu.VMEM)] * 3,
+        out_specs=[pl.BlockSpec(memory_space=pltpu.VMEM)] * 2,
+        scratch_shapes=[
+            pltpu.VMEM((block, columns), STORED),
+            pltpu.VMEM((SLOTS, FETCHED, columns), jnp.bfloat16),
+            pltpu.VMEM((sections, 2 * rows, width), jnp.bfloat16),
+            pltpu.VMEM((sections, *message), f32),
+            pltpu.VMEM((max(groups, depth), *message), f32),
+            pltpu.VMEM((depth, *message), f32),
+            pltpu.VMEM((depth, *message), f32),
+            pltpu.VMEM((rows, width), f32),
+            pltpu.VMEM((groups, rows, part), f32),
+            pltpu.VMEM((faces, *message), f32),
+            pltpu.VMEM((faces, *message), f32),
+            pltpu.VMEM((rows, width), f32),
+            pltpu.VMEM((2, rows, LANES), f32),
+            pltpu.VMEM((depth, rows, LANES), f32),
+            dma((SLOTS,)),
+            dma((2 * depth,)),
+            dma((sections,)),
+            dma((depth,)),
+            dma((depth,)),
+            dma((depth,)),
+            dma((depth,)),
+            dma((faces,)),
+            dma((faces,)),
+            dma((faces,)),
+            dma((faces,)),
+            dma((2 * faces,)),
+            dma((groups,)),
+            dma((depth,)),
+            dma((depth,)),
+        ],
+        compiler_params=pltpu.CompilerParams(
+            collective_id=0, has_side_effects=True, vmem_limit_bytes=VMEM_LIMIT
+        ),
+        cost_estimate=pl.CostEstimate(
+            flops=flops, bytes_accessed=2 * block * columns, transcendentals=0
+        ),
+    )(genotype, centre[None, :], spread[None, :], pheno_probes)
+
+
 def solution(mesh):
     in_specs = (P("samp", "snp"), P("snp"), P("snp"), P(None, ("samp", "snp")))
     out_specs = (P(None, ("samp", "snp")), P(None, "snp"))
@@ -93,6 +612,9 @@
         samples, markers = genotype.shape
 
         def body(*blocks):
+            if fits(mesh, genotype, pheno_probes):
+                sizes = (samples, markers, mesh.shape["samp"], mesh.shape["snp"])
+                return resident(*sizes, *blocks)
             return local(samples, markers, *blocks)
 
         return jax.shard_map(

time: 599 us -> 205 us (0.34)
  waiting for transfers between devices: 315 us -> 0 us
  Pallas kernels: 0 us -> 200 us
  matrix products: 190 us -> 0 us
  blocking collectives: 37.1 us -> 0 us
  other arithmetic: 30.7 us -> 0 us
  between operations: 14.2 us -> 0.64 us
  local copies, waits for them, and re-layouts: 10.3 us -> 3.56 us
    psum x5 -> x0, waiting for transfers between devices: 267 us -> none  [the longest x2 168 us: local(): summed = lax.psum(with_scalars(image, [power]), 'snp')]
    pallas_call x0 -> x1, Pallas kernels: none -> 200 us  [resident(): pl.pallas_call(functools.partial(solve, (samples, markers, faces, columns...]
    dot_general x5 -> x0, matrix products: 190 us -> none  [product(): lax.dot_general(pieces, genotype, (((1,), (dimension,)), ((), ())), prefe...]
    all_gather x1 -> x0, waiting for transfers between devices: 46.8 us -> none  [local(): residual = lax.all_gather(pheno_probes, 'snp', axis=1, tiled=True)]
    psum x1 -> x0, blocking collectives: 37.1 us -> none  [local(): power = lax.psum(power, 'snp')]
    reduce_sum x6 -> x0, other arithmetic: 12 us -> none  [row_sum(): return jnp.sum(values, axis=1, keepdims=True)]
    concatenate x5 -> x0, local copies, waits for them, and re-layouts: 8.42 us -> none  [with_scalars(): return jnp.concatenate([values, *scalars, filler], axis=1)]
  transfers between devices with their start and end apart: 6 -> 0, of which waited for: 6 -> 0; matrix products, arithmetic and copies ran while one was open for 0% -> 0% of each run, Pallas kernels for 0% -> 0%
where the time goes in v1:
time: 205 us
  Pallas kernels  200 us (98%)
  local copies, waits for them, and re-layouts  3.56 us (2%)
    pallas_call x1, Pallas kernels, resident(): pl.pallas_call(functools.partial(solve, (samples, markers, faces, columns...  200 us

profile of v1, /device:TPU:0, one launch (start us, length us, event | category | flops | bytes accessed | tf_op | source)
XLA Modules:
  0.0 204.7 jit_solution(10536213348093099722)
XLA Ops:
  0.6 200.5 %shard_map.59 = (f32[32,1280]{1,0:T(8,128)}, f32[32,5120]{1,0:T(8,128)}) custom-call(bf16[10240,5120]{1,0:T(8,128)(2,1)} %genotype.1, f32[1,5120]{1,0:T(1,128)} %bitcast.2, f32[1,5120]{1,0:T(1,128)} %bitcast.3, f32[32,1280]{1,0:T(8,128)} %pheno.1), custom_call_target="tpu_custom_call" | custom-call | flops 33554432000 | bytes 104857600 | tf_op jit(solution)/shard_map/pallas_call | solution.py:559
  201.1 1.6 copy.8
  202.7 2.0 copy.9

commit v2 on v1

--- a/solution.py
+++ b/solution.py
@@ -90,6 +90,8 @@
 
 MESH = pl.DeviceIdType.MESH
 STORED = jnp.float8_e4m3fn
+SUBLANES = 8
+FACING = 4
 SLOTS = 7
 FETCHED = 64
 VMEM_LIMIT = 67043328
@@ -108,6 +110,21 @@
     wide = high.astype(jnp.float32)
     low = (values - wide).astype(jnp.bfloat16)
     return high, low, wide + low.astype(jnp.float32)
+
+
+def read(ref, slot, rows):
+    blocks = (ref.shape[1] - SUBLANES) // rows
+    return jnp.concatenate([ref[slot, q * rows : (q + 1) * rows, :] for q in range(blocks)], axis=1)
+
+
+def write(ref, slot, values):
+    rows = values.shape[0]
+    for q in range(values.shape[1] // LANES):
+        ref[slot, q * rows : (q + 1) * rows, :] = values[:, q * LANES : (q + 1) * LANES]
+
+
+def tail_of(ref):
+    return pl.ds(ref.shape[1] - SUBLANES, SUBLANES)
 
 
 def lanes_sum(values):
@@ -192,27 +209,40 @@
         return pl.ds(at(slot), width)
 
     lane = lax.broadcasted_iota(jnp.int32, (rows, LANES), 1)
+    diagonal = lane == lax.broadcasted_iota(jnp.int32, (rows, LANES), 0)
+    line = lax.broadcasted_iota(jnp.int32, (SUBLANES, LANES), 0)
+    nothing = jnp.zeros((SUBLANES, LANES), jnp.float32)
 
     def packed(*scalars):
-        block = jnp.zeros((rows, LANES), jnp.float32)
+        tile = nothing
         for position, scalar in enumerate(scalars):
-            block = jnp.where(lane == position, scalar, block)
-        return block
-
-    shards[snp, :, :width] = pheno[...]
-    shards[snp, :, width:] = jnp.zeros((rows, LANES), jnp.float32)
+            turned = jnp.sum(jnp.where(diagonal, scalar, 0.0), axis=0, keepdims=True)
+            tile = jnp.where(line == position, turned, tile)
+        return tile
+
+    def unpacked(tile, position):
+        return row_sum(jnp.where(diagonal, tile[position : position + 1, :], 0.0))
+
+    write(shards, snp, pheno[...])
+    tail = tail_of(shards)
+    shards[snp, tail, :] = nothing
 
     barrier = pltpu.get_barrier_semaphore()
     partners = [to_snp(z, 1 - y), to_samp(x, 1 - core)]
     partners += [to_snp(swap(z, d, depth), y) for d in range(1, depth)]
-    partners += [to_samp(swap(x, d, faces), core) for d in range(1, faces)]
+    partners.append(to_samp(1 - x, core))
     for partner in partners:
         pl.semaphore_signal(barrier, inc=1, device_id=partner, device_id_type=MESH)
 
     per = width // block_rows
     blocks = 2 * depth * per
 
-    def shard_at(step):
+    def step_of(turn):
+        later = jnp.where(turn > depth, turn, turn - 1)
+        return jnp.where(turn < 2, turn, jnp.where(turn == 2, depth, later))
+
+    def shard_at(turn):
+        step = step_of(turn)
         return swap(z, lax.rem(step, depth), depth) * 2 + lax.rem(y + step // depth, 2)
 
     def fetch(index):
@@ -257,24 +287,26 @@
 
         lax.fori_loop(0, per, one, 0)
 
-    def receive_shard(step):
+    def receive_shard(turn):
+        step = step_of(turn)
+
         @pl.when(step > 0)
         def _():
-            shard_arrival(shard_at(step)).wait_recv()
+            shard_arrival(shard_at(turn)).wait_recv()
 
         @pl.when(jnp.logical_and(step > 0, step < depth))
         def _():
             forward(step).start()
 
     def take_shard(slot, sums):
-        values = shards[slot, :, :width]
+        values = read(shards, slot, rows)
         high, low, rounded = pieces_of(values)
         pieces[slot, :rows, :width] = high
         pieces[slot, rows:, :width] = low
         return (
             sums[0] + lanes_sum(rounded),
             sums[1] + lanes_sum(values * values),
-            sums[2] + shards[slot, :, width:],
+            sums[2] + shards[slot, tail, :],
         )
 
     def raw_part(slot, target):
@@ -283,31 +315,23 @@
             stored[row_range(slot), column(target)],
             preferred_element_type=jnp.float32,
         )
-        sent[target, :, :part] += result[:rows] + result[rows:]
+        write(sent, target, read(sent, target, rows) + (result[:rows] + result[rows:]))
 
     def core_send(xx):
         return remote(
             sent.at[xx * 2 + 1 - core], crossed.at[xx], c_send.at[xx], c_recv.at[xx], to_samp(x, 1 - core)
         )
 
-    def face_send(xx):
-        return remote(crossed.at[xx], faced.at[x], x_send.at[xx], x_recv.at[x], to_samp(xx, core))
-
-    def face_arrival(xx):
-        return remote(crossed.at[xx], faced.at[xx], x_send.at[xx], x_recv.at[xx], to_samp(xx, core))
-
-    def own_load_to(d):
-        device = to_samp(swap(x, d, faces), core) if d else to_samp(x, 1 - core)
-        return remote(loads.at[samp], loads.at[samp], lg_send.at[d], lg_recv.at[samp], device)
-
-    def load_forward(d):
-        slot = swap(x, d, faces) * 2 + core
+    def face_exchange(xx, turn):
+        slot = turn * faces + xx
         return remote(
-            loads.at[slot], loads.at[slot], lg_send.at[faces + d], lg_recv.at[slot], to_samp(x, 1 - core)
-        )
-
-    def load_arrival(slot):
-        return remote(loads.at[slot], loads.at[slot], lg_send.at[0], lg_recv.at[slot], to_samp(x, 1 - core))
+            crossed.at[xx], faced.at[slot], x_send.at[xx], x_recv.at[slot], to_samp(1 - x, core)
+        )
+
+    def load_exchange(slot):
+        return remote(
+            loads.at[slot], loads.at[slot], lg_send.at[slot], lg_recv.at[slot], to_samp(x, 1 - core)
+        )
 
     def take_load(slot, sums):
         values = loads[slot]
@@ -366,68 +390,60 @@
             return sums
 
         empty = jnp.zeros((rows, LANES), jnp.float32)
-        last = 2 * depth - 1
-        sums = lax.fori_loop(0, last, one_shard, (empty, empty, empty))
+        last = jnp.int32(2 * depth - 1)
+        sums = lax.fori_loop(0, last, one_shard, (empty, empty, nothing))
         if not counter:
             load_stored(last)
         slot = shard_at(last)
         shard_arrival(slot).wait_recv()
         sums = take_shard(slot, sums)
-        scalars = packed(row_sum(sums[0]), row_sum(sums[1]), sums[2][:, :1])
+        scalars = packed(row_sum(sums[0]), row_sum(sums[1]), unpacked(sums[2], 0))
         for target in range(2 * faces):
-            sent[target, :, part:] = scalars
-        order = [swap(x, d, faces) for d in range(faces - 1, -1, -1)]
+            sent[target, tail, :] = scalars
+        order = [1 - x, x]
         for xx in order:
             raw_part(slot, xx * 2 + 1 - core)
             core_send(xx).start()
         for xx in order:
             raw_part(slot, xx * 2 + core)
-        for xx in order[:-1]:
+        for xx in order:
             core_send(xx).wait_recv()
             crossed[xx] += sent[xx * 2 + core]
-            face_send(xx).start()
-        core_send(x).wait_recv()
-        total = crossed[x] + sent[samp]
-        for xx in order[:-1]:
-            face_arrival(xx).wait_recv()
-            total = total + faced[xx]
-
-        norm_next = total[:, part + 1 : part + 2]
-        load = (total[:, :part] - total[:, part : part + 1] * centre[:, column(samp)]) * (
-            1.0 / spread[:, column(samp)]
-        )
-        if counter:
-            ratio = norm_next / norm
-            cross = total[:, part + 2 : part + 3]
-            load = load + ratio * loads[samp]
-            square = norm_next + 2.0 * ratio * cross + ratio * ratio * square
-            loads[samp] = load
-        else:
-            square = norm_next
-            loads[samp] = load
-        for xx in order[:-1]:
-            face_send(xx).wait_send()
+            face_exchange(xx, counter % 2).start()
         for d in range(depth):
             own_shard_to(d).wait_send()
         for d in range(1, depth):
             forward(d).wait_send()
-        for d in range(faces - 1, -1, -1):
-            own_load_to(d).start()
+        sums = (empty, empty)
+        norm_next = None
+        for xx in order:
+            arrival = face_exchange(xx, counter % 2)
+            arrival.wait_recv()
+            slot = xx * 2 + core
+            where = faced.at[counter % 2 * faces + xx]
+            if norm_next is None:
+                scalars = crossed[xx, tail, :] + where[tail, :]
+                offset, norm_next = unpacked(scalars, 0), unpacked(scalars, 1)
+                if counter:
+                    ratio = norm_next / norm
+                    cross = unpacked(scalars, 2)
+                    square = norm_next + 2.0 * ratio * cross + ratio * ratio * square
+                else:
+                    square = norm_next
+            total = read(crossed, xx, rows) + read(faced, counter % 2 * faces + xx, rows)
+            load = (total - offset * centre[:, column(slot)]) * (1.0 / spread[:, column(slot)])
+            loads[slot] = load + ratio * loads[slot] if counter else load
+            arrival.wait_send()
+            load_exchange(slot).start()
+            sums = take_load(slot, sums)
         if counter:
-            direction[...] = shards[snp, :, :width] + ratio * direction[...]
+            direction[...] = read(shards, snp, rows) + ratio * direction[...]
         else:
-            direction[...] = shards[snp, :, :width]
+            direction[...] = read(shards, snp, rows)
         norm = norm_next
-
-        sums = take_load(samp, (empty, empty))
-        for d in range(1, faces):
-            other = swap(x, d, faces) * 2 + core
-            load_arrival(other).wait_recv()
-            load_forward(d).start()
-            sums = take_load(other, sums)
-        for d in range(faces):
-            other = swap(x, d, faces) * 2 + 1 - core
-            load_arrival(other).wait_recv()
+        for xx in order:
+            other = xx * 2 + 1 - core
+            load_exchange(other).wait_recv()
             sums = take_load(other, sums)
         power = row_sum(sums[1])
 
@@ -451,15 +467,15 @@
 
                 @pl.when(jnp.logical_not(own))
                 def _():
-                    sent[zz, :, :width] = own_image[...]
-                    sent[zz, :, width:] = scalars
+                    write(sent, zz, own_image[...])
+                    sent[zz, tail, :] = scalars
                     pair_send(zz).start()
 
                 @pl.when(own)
                 def _():
                     pair_send(zz).wait_recv()
-                    paired[zz, :, :width] += own_image[...]
-                    paired[zz, :, width:] += scalars
+                    write(paired, zz, read(paired, zz, rows) + own_image[...])
+                    paired[zz, tail, :] += scalars
 
                 @pl.when(jnp.logical_and(own, index < 2 * depth - 1))
                 def _():
@@ -468,19 +484,20 @@
                 return carry
 
             lax.fori_loop(0, 2 * depth, one_image, 0)
-            total = paired[z]
+            total, scalars = read(paired, z, rows), paired[z, tail, :]
             for d in range(depth - 1, 0, -1):
                 zz = swap(z, d, depth)
                 far_arrival(zz).wait_recv()
-                total = total + gathered[zz]
-            power = total[:, width : width + 1]
+                total = total + read(gathered, zz, rows)
+                scalars = scalars + gathered[zz, tail, :]
+            power = unpacked(scalars, 0)
             step = norm / (power / markers + RIDGE * square)
             own_direction = direction[...]
             update = step * own_direction
-            applied = total[:, :width] / markers + RIDGE * own_direction
-            residual = shards[snp, :, :width] - step * applied
-            shards[snp, :, :width] = residual
-            shards[snp, :, width:] = packed(row_sum(residual * own_direction))
+            applied = total / markers + RIDGE * own_direction
+            residual = read(shards, snp, rows) - step * applied
+            write(shards, snp, residual)
+            shards[snp, tail, :] = packed(row_sum(residual * own_direction))
             solution[...] = update if not counter else solution[...] + update
             for d in range(depth):
                 pair_send(swap(z, d, depth)).wait_send()
@@ -521,10 +538,8 @@
                 spread_power(d, z).wait_send()
             for xx in order:
                 core_send(xx).wait_send()
-        for d in range(faces):
-            own_load_to(d).wait_send()
-        for d in range(1, faces):
-            load_forward(d).wait_send()
+        for xx in range(faces):
+            load_exchange(xx * 2 + core).wait_send()
 
 
 def power_of_two(count):
@@ -539,9 +554,9 @@
     rows = pheno_probes.shape[0]
     block, columns = samples // groups, markers // sections
     width, part = block // sections, columns // groups
-    if rows % 16 or width % LANES or width != part or sections // 2 < groups or groups < 4:
+    if rows % 16 or width % LANES or width != part or sections // 2 < groups or groups != FACING:
         return False
-    shard = rows * (width + LANES) * 4
+    shard = rows * width * 4 + SUBLANES * LANES * 4
     used = block * columns + SLOTS * FETCHED * columns * 2 + sections * rows * width * 4
     used += (sections + 3 * sections // 2 + 2 * groups + 6) * shard
     return used < VMEM_LIMIT
@@ -552,7 +567,7 @@
     block, columns = genotype.shape
     faces, depth = groups // 2, sections // 2
     part = columns // groups
-    message = (rows, width + LANES)
+    message = (rows * width // LANES + SUBLANES, LANES)
     f32 = jnp.float32
     dma = pltpu.SemaphoreType.DMA
     flops = 2 * (2 * ROUNDS - 1) * 2 * rows * block * columns
@@ -575,7 +590,7 @@
             pltpu.VMEM((rows, width), f32),
             pltpu.VMEM((groups, rows, part), f32),
             pltpu.VMEM((faces, *message), f32),
-            pltpu.VMEM((faces, *message), f32),
+            pltpu.VMEM((2 * faces, *message), f32),
             pltpu.VMEM((rows, width), f32),
             pltpu.VMEM((2, rows, LANES), f32),
             pltpu.VMEM((depth, rows, LANES), f32),
@@ -589,8 +604,8 @@
             dma((faces,)),
             dma((faces,)),
             dma((faces,)),
-            dma((faces,)),
             dma((2 * faces,)),
+            dma((groups,)),
             dma((groups,)),
             dma((depth,)),
             dma((depth,)),

time: 205 us -> 192 us (0.937)
  Pallas kernels: 200 us -> 188 us
    pallas_call x1, Pallas kernels: 200 us -> 188 us  [resident(): pl.pallas_call(functools.partial(solve, (samples, markers, faces, columns...]
where the time goes in v2:
time: 192 us
  Pallas kernels  188 us (98%)
  local copies, waits for them, and re-layouts  3.56 us (2%)
    pallas_call x1, Pallas kernels, resident(): pl.pallas_call(functools.partial(solve, (samples, markers, faces, columns...  188 us

profile of v2, /device:TPU:0, one launch (start us, length us, event | category | flops | bytes accessed | tf_op | source)
XLA Modules:
  0.0 191.8 jit_solution(9373638730478275758)
XLA Ops:
  0.6 187.6 %shard_map.59 = (f32[32,1280]{1,0:T(8,128)}, f32[32,5120]{1,0:T(8,128)}) custom-call(bf16[10240,5120]{1,0:T(8,128)(2,1)} %genotype.1, f32[1,5120]{1,0:T(1,128)} %bitcast.2, f32[1,5120]{1,0:T(1,128)} %bitcast.3, f32[32,1280]{1,0:T(8,128)} %pheno.1), custom_call_target="tpu_custom_call" | custom-call | flops 33554432000 | bytes 104857600 | tf_op jit(solution)/shard_map/pallas_call | solution.py:574
  188.3 1.6 copy.8
  189.9 2.0 %copy.9 = f32[32,5120]{1,0:T(8,128)} copy(f32[32,5120]{1,0:T(8,128)} %get-tuple-element.5) | data formatting | bytes 1310720
